TPU v7x, 512 devices: a 8x2x16 block of a 8x8x16 slice. The times are simulated.
512 devices in a mesh: groups: 2 (over y), expert: 128 (over z, x), tensor: 2 (over core).
Axes of the slice: x: 8, y: 2, z: 16, core: 2. Of those that a mesh axis runs over, the one named last changes fastest.
The devices are a block of a 8x8x16 slice.
Arguments:
- tokens: bfloat16 [16384, 1536], P(('groups', 'expert')), parts along dimension 0, may hold values from -12 to 12
- gain: float32 [1536], replicated, may hold values from 0.25 to 1.75
- route_ids: int32 [16384, 4], P(('groups', 'expert')), parts along dimension 0, may hold values from 0 to 63, as said below
- route_weights: float32 [16384, 4], P(('groups', 'expert')), parts along dimension 0, may hold values from 0.05 to 0.5
- w_gate: bfloat16 [128, 1536, 768], P('expert', None, 'tensor'), may hold values from -0.15625 to 0.15625
- w_up: bfloat16 [128, 1536, 768], P('expert', None, 'tensor'), may hold values from -0.15625 to 0.15625
- w_down: bfloat16 [128, 768, 1536], P('expert', 'tensor'), may hold values from -0.15625 to 0.15625
Outputs:
- mixed: bfloat16 [16384, 1536], P(('groups', 'expert')), parts along dimension 0
There are 2 independent parts, one for each index of `groups`. A program takes and returns all parts, laid end to end along the dimension named above; an argument that names none is the same for every part. Nothing has to cross between parts.
Inputs may be any that keep to these rules, and one draw needn't show every extreme that they name: `route_ids`: each row names 4 different experts. In each aligned block of 32 rows no expert is named more than 2 times; one expert, the same in every block, is named exactly 2 times in every block, and the other experts' counts within a block differ by at most one.
All inputs are finite; a program needn't handle non-finite values.
Results may differ from a plain program's by a relative error of at most 0.0045.
Values may be sent and summed in bfloat16 or wider, within the bound.
No kernel may reach another device: no remote copies, remote signals or barrier semaphores. Data moves between devices by JAX's collectives and lax.ppermute only.
A program may use at most 64 MiB of HBM per device.

v0:
```python
import jax
import jax.numpy as jnp
from jax import lax
from jax.sharding import PartitionSpec as P


def joined_along(pieces, dim):
    lengths = list(pieces.shape[1:])
    lengths[dim] *= pieces.shape[0]
    return jnp.moveaxis(pieces, 0, dim).reshape(lengths)


def copy_for_each(array, axis):
    devices = lax.axis_size(axis)
    return lax.all_to_all(
        jnp.broadcast_to(array[None], (devices, *array.shape)), axis, 0, 0, tiled=True
    )


def gathered_copies(array, axis, dim):
    return joined_along(copy_for_each(array, axis), dim)


def in_blocks(array, dim, devices):
    lengths = array.shape
    pieces = array.reshape(*lengths[:dim], devices, lengths[dim] // devices, *lengths[dim + 1 :])
    return jnp.moveaxis(pieces, dim, 0)


def sent_and_summed(array, axis, dim):
    devices = lax.axis_size(axis)
    pieces = lax.all_to_all(in_blocks(array, dim, devices), axis, 0, 0, tiled=True)
    return jnp.sum(pieces, axis=0)


def gated_unit(gate_val, up_val):
    return gate_val * jax.nn.sigmoid(1.702 * gate_val) * (up_val + 1.0)


def route_tables(chosen_ids, chosen_weights, expert_count, slot_room):
    row_count, top_count = chosen_ids.shape
    matches = (chosen_ids[:, :, None] == jnp.arange(expert_count, dtype=jnp.int32)).astype(
        jnp.float32
    )
    flat_match = matches.reshape(row_count * top_count, expert_count)
    order_range = jnp.arange(row_count * top_count, dtype=jnp.int32)
    earlier = (order_range[:, None] > order_range[None, :]).astype(jnp.float32)
    before = jnp.dot(
        earlier, flat_match, precision=lax.Precision.HIGHEST, preferred_element_type=jnp.float32
    )
    position = jnp.sum(before * flat_match, axis=1).reshape(row_count, top_count).astype(jnp.int32)
    slot_index = chosen_ids * slot_room + position
    targets = jnp.arange(expert_count * slot_room, dtype=jnp.int32)
    slot_hits = slot_index[None, :, :] == targets[:, None, None]
    send_table = jnp.sum(slot_hits.astype(jnp.float32), axis=2).astype(jnp.bfloat16)
    mix_table = jnp.sum(jnp.where(slot_hits, chosen_weights[None, :, :], 0.0), axis=2)
    return (send_table, mix_table)


def per_device(tokens, gain, route_ids, route_weights, w_gate, w_up, w_down):
    expert_axis = lax.axis_size("expert")
    expert_count = expert_axis // 2
    tensor_count = lax.axis_size("tensor")
    own_rows = tokens.shape[0] // tensor_count
    top_count = route_ids.shape[1]
    capacity = max(2, own_rows * top_count // expert_count)
    gate_local = w_gate[0]
    up_local = w_up[0]
    down_local = w_down[0]
    first_row = lax.axis_index("tensor") * own_rows
    own_tokens = lax.dynamic_slice_in_dim(tokens, first_row, own_rows, 0)
    own_ids = lax.dynamic_slice_in_dim(route_ids, first_row, own_rows, 0)
    own_weights = lax.dynamic_slice_in_dim(route_weights, first_row, own_rows, 0)
    resident = own_tokens.astype(jnp.float32)
    inv_rms = lax.rsqrt(jnp.mean(resident * resident, axis=1, keepdims=True) + 1e-05)
    normed = (resident * inv_rms * gain).astype(jnp.bfloat16)
    send_table, mix_table = route_tables(own_ids, own_weights, expert_count, capacity)
    packed = jnp.dot(send_table, normed, preferred_element_type=jnp.float32).astype(jnp.bfloat16)
    features = packed.shape[1]
    by_expert = packed.reshape(expert_count, 1, capacity, features)
    outgoing = jnp.broadcast_to(by_expert, (expert_count, 2, capacity, features)).reshape(
        expert_axis * capacity, features
    )
    arrived = lax.all_to_all(outgoing, "expert", split_axis=0, concat_axis=0, tiled=True)
    row_piece = gathered_copies(arrived, "tensor", 0)
    gate_val = jnp.dot(row_piece, gate_local, preferred_element_type=jnp.float32)
    up_val = jnp.dot(row_piece, up_local, preferred_element_type=jnp.float32)
    hidden = gated_unit(gate_val, up_val).astype(jnp.bfloat16)
    partial_value = sent_and_summed(
        jnp.dot(hidden, down_local, preferred_element_type=jnp.float32), "tensor", 0
    )
    returned = lax.all_to_all(
        partial_value.astype(jnp.bfloat16), "expert", split_axis=0, concat_axis=0, tiled=True
    ).astype(partial_value.dtype)
    expert_out = (
        returned.reshape(expert_count, 2, capacity, features)
        .sum(axis=1)
        .reshape(expert_count * capacity, features)
    )
    weighted = jnp.dot(
        mix_table.T, expert_out, precision=lax.Precision.HIGHEST, preferred_element_type=jnp.float32
    )
    finished = (resident + weighted).astype(jnp.bfloat16)
    return gathered_copies(finished, "tensor", 0)


def solution(mesh):
    placed = (
        P(("groups", "expert"), None),
        P(),
        P(("groups", "expert"), None),
        P(("groups", "expert"), None),
        P("expert", None, "tensor"),
        P("expert", None, "tensor"),
        P("expert", "tensor", None),
    )
    return jax.shard_map(
        per_device,
        mesh=mesh,
        in_specs=placed,
        out_specs=P(("groups", "expert"), None),
        check_vma=False,
    )
```

profile of v0, /device:TPU:65, one launch (start us, length us, event | category | flops | bytes accessed | tf_op | source)
XLA Modules:
  0.0 179.2 jit_solution(15526253094269792175)
XLA Ops:
  0.0 0.0 copy-start
  0.0 1.1 fusion.9
  1.1 0.8 constant_dynamic-slice_fusion.1
  1.9 0.8 constant_dynamic-slice_fusion
  2.6 0.1 copy.19
  2.7 0.1 eq.30
  2.8 0.2 fusion.8
  3.0 0.1 convert_element_type.46
  3.1 0.1 copy.15
  3.2 0.1 convert_reduce_fusion.1
  3.3 1.2 convolution_convert_fusion
  4.6 0.1 broadcast_in_dim.24
  4.7 0.4 broadcast_in_dim.25
  5.1 91.8 %all_to_all.30 = bf16[128,2,1536]{2,1,0:T(2,128)(2,1)S(1)} all-to-all(bf16[128,2,1536]{2,1,0:T(2,128)(2,1)S(1)} %bitcast.23), channel_id=1, replica_groups=mesh['groups'=2,'expert'=128,'tensor'=2] {'expert'}, dimensions={0} | all-to-all | bytes 1572864 | tf_op jit(solution)/shard_map/all_to_all | solution.py:84
  96.9 0.3 broadcast_in_dim.26
  97.2 0.1 broadcast_in_dim.27
  97.3 0.0 copy-start.2
  97.3 9.0 %all_to_all.31 = bf16[2,256,1536]{2,1,0:T(8,128)(2,1)S(1)} all-to-all(bf16[2,256,1536]{2,1,0:T(8,128)(2,1)S(1)} %broadcast_in_dim.27), channel_id=1, replica_groups=mesh['groups'=2,'expert'=128,'tensor'=2] {'tensor'}, dimensions={0} | all-to-all | bytes 3145728 | tf_op jit(solution)/shard_map/all_to_all | solution.py:15
  106.3 0.0 copy-done.2
  106.3 0.0 copy-start.3
  106.3 1.0 fusion.6
  107.3 0.3 copy-done.3
  107.6 1.0 fusion.2
  108.6 0.0 copy-done
  108.6 1.0 fusion.3
  109.6 7.2 %all_to_all.32 = f32[2,256,1536]{2,1,0:T(8,128)} all-to-all(f32[2,256,1536]{2,1,0:T(8,128)S(1)} %fusion.3), channel_id=1, replica_groups=mesh['groups'=2,'expert'=128,'tensor'=2] {'tensor'}, dimensions={0} | all-to-all | bytes 6291456 | tf_op jit(solution)/shard_map/all_to_all | solution.py:32
  116.9 2.2 %reduce_sum.58 = bf16[256,1536]{1,0:T(8,128)(2,1)S(1)} reduce(f32[2,256,1536]{2,1,0:T(8,128)} %all_to_all.32, f32[]{:T(128)} %constant.7.clone.1), dimensions={0}, to_apply=%region_4.5 | reduce | flops 393216 | bytes 3932164 | tf_op jit(solution)/shard_map/reduce_sum | solution.py:33
  119.1 0.3 convert_element_type.53
  119.4 49.4 %all_to_all.33 = bf16[128,2,1536]{2,1,0:T(2,128)(2,1)S(1)} all-to-all(bf16[128,2,1536]{2,1,0:T(2,128)(2,1)S(1)} %convert_element_type.53), channel_id=1, replica_groups=mesh['groups'=2,'expert'=128,'tensor'=2] {'expert'}, dimensions={0} | all-to-all | bytes 1572864 | tf_op jit(solution)/shard_map/all_to_all | solution.py:92
  168.7 0.0 copy-start.1
  168.7 1.0 convert_reduce_fusion
  169.7 0.5 reshape.47
  170.3 0.0 copy-done.1
  170.3 0.5 fusion
  170.8 7.7 %all_to_all.34 = bf16[2,32,1536]{2,1,0:T(8,128)(2,1)S(1)} all-to-all(bf16[2,32,1536]{2,1,0:T(8,128)(2,1)S(1)} %broadcast_in_dim.48), channel_id=1, replica_groups=mesh['groups'=2,'expert'=128,'tensor'=2] {'tensor'}, dimensions={0} | all-to-all | bytes 393216 | tf_op jit(solution)/shard_map/all_to_all | solution.py:15
  178.5 0.7 copy.21
  (4 shorter events, 0.0 us)
Async XLA Ops:
  0.0 108.6 %copy-start = (bf16[1,384,1536]{2,1,0:T(8,128)(2,1)S(1)}, bf16[1,384,1536]{2,1,0:T(8,128)(2,1)}, u32[]{:S(2)}) copy-start(bf16[1,384,1536]{2,1,0:T(8,128)(2,1)} %param.13) | copy-start | bytes 3538948
  97.3 9.0 %copy-start.2 = (bf16[1,1536,384]{2,1,0:T(8,128)(2,1)S(1)}, bf16[1,1536,384]{2,1,0:T(8,128)(2,1)}, u32[]{:S(2)}) copy-start(bf16[1,1536,384]{2,1,0:T(8,128)(2,1)} %param.11) | copy-start | bytes 3538948
  106.3 1.3 copy-start.3
  168.7 1.5 copy-start.1
where the time goes:
time: 180 us; the launch traced here: 179 us
  blocking collectives  165 us (92%)
  matrix products  4.91 us (3%)
  local copies, waits for them, and re-layouts  4.67 us (3%)
  other arithmetic  4.41 us (2%)
    all_to_all x1, blocking collectives, per_device(): lax.all_to_all(outgoing, 'expert', split_axis=0, concat_axis=0, tiled=True)  91.8 us
    all_to_all x1, blocking collectives, per_device(): lax.all_to_all(partial_value.astype(jnp.bfloat16), 'expert', split_axis=0...  49.4 us
    all_to_all x2, blocking collectives, copy_for_each(): lax.all_to_all(jnp.broadcast_to(array[None], (devices, *array.shape)), ax...  16.7 us
    all_to_all x1, blocking collectives, sent_and_summed(): lax.all_to_all(in_blocks(array, dim, devices), axis, 0, 0, tiled=True)  7.24 us

commit v1 on v0

v1 whole, which is shorter than its diff:
```python
import jax
import jax.numpy as jnp
import numpy as np
from jax import lax
from jax.sharding import Mesh, PartitionSpec as P

X = 8


def gated_unit(gate_val, up_val):
    return gate_val * jax.nn.sigmoid(1.702 * gate_val) * (up_val + 1.0)


def route_tables(ids, weights, experts, room):
    rows, top = ids.shape
    matches = (ids[:, :, None] == jnp.arange(experts, dtype=jnp.int32)).astype(jnp.bfloat16)
    named = jnp.sum(matches, axis=1)
    earlier = (jnp.arange(rows)[:, None] > jnp.arange(rows)[None, :]).astype(jnp.bfloat16)
    before = jnp.dot(earlier, named, preferred_element_type=jnp.float32)
    position = jnp.sum(before[:, None, :] * matches.astype(jnp.float32), axis=2).astype(jnp.int32)
    slot = ids * room + position
    targets = jnp.arange(experts * room, dtype=jnp.int32)
    hits = slot[None, :, :] == targets[:, None, None]
    send = jnp.sum(hits.astype(jnp.float32), axis=2).astype(jnp.bfloat16)
    mix = jnp.sum(jnp.where(hits, weights[None, :, :], 0.0), axis=2)
    return send, mix


def per_device(tokens, gain, route_ids, route_weights, w_gate, w_up, w_down):
    zs = lax.axis_size("z")
    xs = lax.axis_size("x")
    cores = lax.axis_size("tensor")
    experts = zs * xs // 2
    pairs = xs // 2
    own = tokens.shape[0] // cores
    feats = tokens.shape[1]
    room = max(2, own * route_ids.shape[1] // experts)
    first = lax.axis_index("tensor") * own
    own_tokens = lax.dynamic_slice_in_dim(tokens, first, own, 0)
    own_ids = lax.dynamic_slice_in_dim(route_ids, first, own, 0)
    own_weights = lax.dynamic_slice_in_dim(route_weights, first, own, 0)
    resident = own_tokens.astype(jnp.float32)
    inv_rms = lax.rsqrt(jnp.mean(resident * resident, axis=1, keepdims=True) + 1e-05)
    normed = (resident * inv_rms * gain).astype(jnp.bfloat16)
    send, mix = route_tables(own_ids, own_weights, experts, room)
    slots = experts * room
    packed = jnp.dot(send, normed, preferred_element_type=jnp.float32).astype(jnp.bfloat16)
    arrived = lax.all_to_all(packed, "z", 0, 0, tiled=True)
    order = np.arange(slots).reshape(zs, pairs, room).transpose(1, 0, 2).reshape(pairs, 1, zs * room)
    order = np.broadcast_to(order, (pairs, 2, zs * room)).reshape(-1)
    spread = jnp.asarray(order[:, None] == np.arange(slots)[None, :], jnp.bfloat16)
    outgoing = jnp.dot(spread, arrived, preferred_element_type=jnp.float32).astype(jnp.bfloat16)
    rows = lax.all_to_all(outgoing, "x", 0, 0, tiled=True)
    swap = [(0, 1), (1, 0)]
    other = lax.ppermute(rows, "tensor", swap)
    both = jnp.concatenate([rows, other], axis=0)
    gate_val = jnp.dot(both, w_gate[0], preferred_element_type=jnp.float32)
    up_val = jnp.dot(both, w_up[0], preferred_element_type=jnp.float32)
    hidden = gated_unit(gate_val, up_val).astype(jnp.bfloat16)
    partial = jnp.dot(hidden, w_down[0], preferred_element_type=jnp.float32)
    n = rows.shape[0]
    theirs = lax.ppermute(partial[n:].astype(jnp.bfloat16), "tensor", swap)
    mine = (partial[:n] + theirs.astype(jnp.float32)).astype(jnp.bfloat16)
    back = lax.all_to_all(mine, "x", 0, 0, tiled=True)
    gathered = jnp.dot(spread.T, back, preferred_element_type=jnp.float32).astype(jnp.bfloat16)
    returned = lax.all_to_all(gathered, "z", 0, 0, tiled=True)
    weighted = jnp.dot(
        mix.T, returned.astype(jnp.float32), precision=lax.Precision.HIGHEST, preferred_element_type=jnp.float32
    )
    finished = (resident + weighted).astype(jnp.bfloat16)
    theirs_done = lax.ppermute(finished, "tensor", swap)
    low = lax.axis_index("tensor") == 0
    return jnp.concatenate(
        [jnp.where(low, finished, theirs_done), jnp.where(low, theirs_done, finished)], axis=0
    )


def solution(mesh):
    grid = Mesh(
        mesh.devices.reshape(mesh.devices.shape[0], -1, X, mesh.devices.shape[2]),
        ("groups", "z", "x", "tensor"),
    )
    rows = P(("groups", "z", "x"), None)
    placed = (
        rows,
        P(),
        rows,
        rows,
        P(("z", "x"), None, "tensor"),
        P(("z", "x"), None, "tensor"),
        P(("z", "x"), "tensor", None),
    )
    return jax.shard_map(
        per_device, mesh=grid, in_specs=placed, out_specs=rows, check_vma=False
    )
```

time: 180 us -> 186 us (1.033)
  blocking collectives: 165 us -> 140 us
  starting transfers between devices: 0 us -> 21.9 us
  matrix products: 4.91 us -> 9.94 us
  waiting for transfers between devices: 0 us -> 4.7 us
    all_to_all x5 -> x4, blocking collectives: 165 us -> 140 us  [the longest x1 61.8 us: per_device(): arrived = lax.all_to_all(packed, 'z', 0, 0, tiled=True)]
    ppermute x0 -> x3, starting transfers between devices: none -> 21.9 us  [the longest x1 10.4 us: per_device(): other = lax.ppermute(rows, 'tensor', swap)]
    dot_general x6 -> x7, matrix products: 4.91 us -> 9.94 us  [the longest x1 4.87 us: per_device(): partial = jnp.dot(hidden, w_down[0], preferred_element_type=jnp.float32)]
    ppermute x0 -> x3, waiting for transfers between devices: none -> 4.7 us  [the longest x1 1.89 us: per_device(): theirs = lax.ppermute(partial[n:].astype(jnp.bfloat16), 'tensor', swap)]
    reduce_sum x3, other arithmetic: 3.27 us -> 0.35 us  [the longest x1 0.16 us: route_tables(): jnp.sum(before[:, None, :] * matches.astype(jnp.float32), axis=2)]
  transfers between devices with their start and end apart: 0 -> 3, of which waited for: 0 -> 3; matrix products, arithmetic and copies ran while one was open for 0% -> 0% of each run, Pallas kernels for 0% -> 0%
where the time goes in v1:
time: 186 us; the launch traced here: 185 us
  blocking collectives  140 us (75%)
  starting transfers between devices  21.9 us (12%)
  matrix products  9.94 us (5%)
  waiting for transfers between devices  4.7 us (3%)
  other arithmetic  4.56 us (2%)
  local copies, waits for them, and re-layouts  3.91 us (2%)
    all_to_all x1, blocking collectives, per_device(): arrived = lax.all_to_all(packed, 'z', 0, 0, tiled=True)  61.8 us
    all_to_all x1, blocking collectives, per_device(): returned = lax.all_to_all(gathered, 'z', 0, 0, tiled=True)  29.3 us
    all_to_all x1, blocking collectives, per_device(): back = lax.all_to_all(mine, 'x', 0, 0, tiled=True)  26.2 us
    all_to_all x1, blocking collectives, per_device(): rows = lax.all_to_all(outgoing, 'x', 0, 0, tiled=True)  22.6 us
    ppermute x1, starting transfers between devices, per_device(): other = lax.ppermute(rows, 'tensor', swap)  10.4 us
    ppermute x1, starting transfers between devices, per_device(): theirs_done = lax.ppermute(finished, 'tensor', swap)  9.18 us
    dot_general x1, matrix products, per_device(): partial = jnp.dot(hidden, w_down[0], preferred_element_type=jnp.float32)  4.87 us
  transfers between devices with their start and end apart: 3, of which 3 were waited for; matrix products, arithmetic and copies ran while one was open for 0% of the time, Pallas kernels for 0%

profile of v1, /device:TPU:65, one launch (start us, length us, event | category | flops | bytes accessed | tf_op | source)
XLA Modules:
  0.0 184.9 jit_solution(10546162203846940510)
XLA Ops:
  0.0 0.0 copy-start
  0.0 1.1 fusion.17
  1.1 0.8 constant_dynamic-slice_fusion.1
  1.9 0.8 constant_dynamic-slice_fusion
  2.6 0.1 fusion.25
  2.7 0.1 fusion.26
  2.9 0.2 multiply_reduce_fusion
  3.0 0.8 convert_add_fusion
  3.8 0.1 convert_reduce_fusion
  3.9 1.2 fusion
  5.1 61.8 %all_to_all.48 = bf16[16,8,1536]{2,1,0:T(8,128)(2,1)S(1)} all-to-all(bf16[16,8,1536]{2,1,0:T(8,128)(2,1)S(1)} %fusion), channel_id=1, replica_groups=mesh['groups'=2,'z'=16,'x'=8,'tensor'=2] {'z'}, dimensions={0} | all-to-all | bytes 786432 | tf_op jit(solution)/shard_map/all_to_all | solution.py:48
  66.9 0.0 copy-start.3
  66.9 1.3 convolution_convert_fusion
  68.2 22.6 %all_to_all.49 = bf16[8,32,1536]{2,1,0:T(8,128)(2,1)S(1)} all-to-all(bf16[8,32,1536]{2,1,0:T(8,128)(2,1)S(1)} %bitcast.38), channel_id=1, replica_groups=mesh['groups'=2,'z'=16,'x'=8,'tensor'=2] {'x'}, dimensions={0} | all-to-all | bytes 1572864 | tf_op jit(solution)/shard_map/all_to_all | solution.py:53
  90.8 0.0 copy-start.4
  90.8 10.4 %collective-permute-start = (bf16[256,1536]{1,0:T(8,128)(2,1)S(1)}, bf16[256,1536]{1,0:T(8,128)(2,1)S(1)}, u32[]{:S(2)}, u32[]{:S(2)}) collective-permute-start(bf16[256,1536]{1,0:T(8,128)(2,1)S(1)} %bitcast.40), channel_id=1, source_target_pairs={{0,1},{1,0},{2,3},{3,2},{4,5},{5,4},{6,7},{7,6},{8,9},{9,8},{10,11... | collective-permute-start | bytes 2359304 | tf_op jit(solution)/shard_map/ppermute | solution.py:55
  101.2 1.9 %collective-permute-done = bf16[256,1536]{1,0:T(8,128)(2,1)S(1)} collective-permute-done((bf16[256,1536]{1,0:T(8,128)(2,1)S(1)}, bf16[256,1536]{1,0:T(8,128)(2,1)S(1)}, u32[]{:S(2)}, u32[]{:S(2)}) %collective-permute-start) | collective-permute-done | bytes 786464 | tf_op jit(solution)/shard_map/ppermute | solution.py:55
  103.1 0.0 copy-start.5
  103.1 0.9 copy-done.5
  104.0 0.0 copy-done.3
  104.0 1.9 %fusion.7 = f32[512,384]{1,0:T(8,128)} fusion(bf16[1,1536,384]{2,1,0:T(8,128)(2,1)S(1)} %copy-done.3, bf16[256,1536]{1,0:T(8,128)(2,1)S(1)} %collective-permute-done, bf16[256,1536]{1,0:T(8,128)(2,1)S(1)} %bitcast.41), kind=kOutput, calls=%fused_computation.15 | convolution fusion | flops 607125504 | bytes 3538944 | tf_op jit(solution)/shard_map/dot_general | solution.py:57
  105.8 0.0 copy-done
  105.8 0.0 copy-done.4
  105.8 4.9 %fusion.4 = f32[512,1536]{1,0:T(8,128)} fusion(bf16[1,384,1536]{2,1,0:T(8,128)(2,1)S(1)} %copy-done, f32[512,384]{1,0:T(8,128)} %fusion.7, bf16[1,1536,384]{2,1,0:T(8,128)(2,1)S(1)} %copy-done.4, bf16[256,1536]{1,0:T(8,128)(2,1)} %copy-done.5, bf16[256,1536]{1,0:T(8,128)(2,1)S(1)} %bitcast.42), kind=kOutput, calls=%fused_computation.12 | convolution fusion | flops 1212678144 | bytes 7864320 | tf_op jit(solution)/shard_map/dot_general | solution.py:60
  110.7 1.5 slice.15
  112.2 2.3 %collective-permute-start.1 = (bf16[256,1536]{1,0:T(8,128)(2,1)S(1)}, bf16[256,1536]{1,0:T(8,128)(2,1)S(1)}, u32[]{:S(2)}, u32[]{:S(2)}) collective-permute-start(bf16[256,1536]{1,0:T(8,128)(2,1)S(1)} %slice.15), channel_id=1, source_target_pairs={{0,1},{1,0},{2,3},{3,2},{4,5},{5,4},{6,7},{7,6},{8,9},{9,8},{10,11... | collective-permute-start | bytes 2359304 | tf_op jit(solution)/shard_map/ppermute | solution.py:62
  114.5 1.9 %collective-permute-done.1 = bf16[256,1536]{1,0:T(8,128)(2,1)S(1)} collective-permute-done((bf16[256,1536]{1,0:T(8,128)(2,1)S(1)}, bf16[256,1536]{1,0:T(8,128)(2,1)S(1)}, u32[]{:S(2)}, u32[]{:S(2)}) %collective-permute-start.1) | collective-permute-done | bytes 786464 | tf_op jit(solution)/shard_map/ppermute | solution.py:62
  116.4 1.6 fusion.3
  118.0 0.0 copy-start.2
  118.0 0.0 copy-start.1
  118.1 26.2 %all_to_all.50 = bf16[8,32,1536]{2,1,0:T(8,128)(2,1)S(1)} all-to-all(bf16[8,32,1536]{2,1,0:T(8,128)(2,1)S(1)} %bitcast.39), channel_id=1, replica_groups=mesh['groups'=2,'z'=16,'x'=8,'tensor'=2] {'x'}, dimensions={0} | all-to-all | bytes 1572864 | tf_op jit(solution)/shard_map/all_to_all | solution.py:64
  144.2 0.0 copy-done.2
  144.2 0.3 fusion.1
  144.5 29.3 %all_to_all.51 = bf16[16,8,1536]{2,1,0:T(8,128)(2,1)S(1)} all-to-all(bf16[16,8,1536]{2,1,0:T(8,128)(2,1)S(1)} %fusion.1), channel_id=1, replica_groups=mesh['groups'=2,'z'=16,'x'=8,'tensor'=2] {'z'}, dimensions={0} | all-to-all | bytes 786432 | tf_op jit(solution)/shard_map/all_to_all | solution.py:66
  173.8 0.0 copy-done.1
  173.8 0.3 fusion.2
  174.1 9.2 %collective-permute-start.2 = (bf16[32,1536]{1,0:T(8,128)(2,1)S(1)}, bf16[32,1536]{1,0:T(8,128)(2,1)S(1)}, u32[]{:S(2)}, u32[]{:S(2)}) collective-permute-start(bf16[32,1536]{1,0:T(8,128)(2,1)S(1)} %fusion.2), channel_id=1, source_target_pairs={{0,1},{1,0},{2,3},{3,2},{4,5},{5,4},{6,7},{7,6},{8,9},{9,8},{10,11... | collective-permute-start | bytes 294920 | tf_op jit(solution)/shard_map/ppermute | solution.py:71
  183.3 0.9 collective-permute-done.2
  184.3 0.7 pad_maximum_fusion.7
  (2 shorter events, 0.0 us)
Async XLA Ops:
  0.0 105.8 %copy-start = (bf16[1,384,1536]{2,1,0:T(8,128)(2,1)S(1)}, bf16[1,384,1536]{2,1,0:T(8,128)(2,1)}, u32[]{:S(2)}) copy-start(bf16[1,384,1536]{2,1,0:T(8,128)(2,1)} %param.14) | copy-start | bytes 3538948
  66.9 37.0 %copy-start.3 = (bf16[1,1536,384]{2,1,0:T(8,128)(2,1)S(1)}, bf16[1,1536,384]{2,1,0:T(8,128)(2,1)}, u32[]{:S(2)}) copy-start(bf16[1,1536,384]{2,1,0:T(8,128)(2,1)} %param.12) | copy-start | bytes 3538948
  90.8 15.0 %copy-start.4 = (bf16[1,1536,384]{2,1,0:T(8,128)(2,1)S(1)}, bf16[1,1536,384]{2,1,0:T(8,128)(2,1)}, u32[]{:S(2)}) copy-start(bf16[1,1536,384]{2,1,0:T(8,128)(2,1)} %param.13) | copy-start | bytes 3538948
  90.8 12.3 %collective-permute-start = (bf16[256,1536]{1,0:T(8,128)(2,1)S(1)}, bf16[256,1536]{1,0:T(8,128)(2,1)S(1)}, u32[]{:S(2)}, u32[]{:S(2)}) collective-permute-start(bf16[256,1536]{1,0:T(8,128)(2,1)S(1)} %bitcast.40), channel_id=1, source_target_pairs={{0,1},{1,0},{2,3},{3,2},{4,5},{5,4},{6,7},{7,6},{8,9},{9,8},{10,11... | collective-permute-start | bytes 2359304 | tf_op jit(solution)/shard_map/ppermute | solution.py:55
  103.1 0.9 copy-start.5
  112.2 4.2 %collective-permute-start.1 = (bf16[256,1536]{1,0:T(8,128)(2,1)S(1)}, bf16[256,1536]{1,0:T(8,128)(2,1)S(1)}, u32[]{:S(2)}, u32[]{:S(2)}) collective-permute-start(bf16[256,1536]{1,0:T(8,128)(2,1)S(1)} %slice.15), channel_id=1, source_target_pairs={{0,1},{1,0},{2,3},{3,2},{4,5},{5,4},{6,7},{7,6},{8,9},{9,8},{10,11... | collective-permute-start | bytes 2359304 | tf_op jit(solution)/shard_map/ppermute | solution.py:62
  118.0 26.2 %copy-start.2 = (bf16[256,128]{1,0:T(8,128)(2,1)S(1)}, bf16[256,128]{1,0:T(8,128)(2,1)}, u32[]{:S(2)}) copy-start(bf16[256,128]{1,0:T(8,128)(2,1)} %constant.27.clone) | copy-start | bytes 196612
  118.0 55.8 %copy-start.1 = (bf16[64,1536]{1,0:T(8,128)(2,1)S(1)}, bf16[64,1536]{1,0:T(8,128)(2,1)}, u32[]{:S(2)}) copy-start(bf16[64,1536]{1,0:T(8,128)(2,1)} %param.8) | copy-start | bytes 589828
  174.1 10.1 %collective-permute-start.2 = (bf16[32,1536]{1,0:T(8,128)(2,1)S(1)}, bf16[32,1536]{1,0:T(8,128)(2,1)S(1)}, u32[]{:S(2)}, u32[]{:S(2)}) collective-permute-start(bf16[32,1536]{1,0:T(8,128)(2,1)S(1)} %fusion.2), channel_id=1, source_target_pairs={{0,1},{1,0},{2,3},{3,2},{4,5},{5,4},{6,7},{7,6},{8,9},{9,8},{10,11... | collective-permute-start | bytes 294920 | tf_op jit(solution)/shard_map/ppermute | solution.py:71
